TPU v7x, 32 devices: a whole 2x2x4 slice. The times are simulated.
32 devices in a mesh: gx: 4 (over z), gy: 8 (over y, x, core).
Axes of the slice: x: 2, y: 2, z: 4, core: 2. Of those that a mesh axis runs over, the one named last changes fastest.
Arguments:
- coarse_map: float32 [4, 8, 2, 128, 128], P('gx', 'gy'), may hold values from -0.675 to 0.675, as said below
- fine_maps: float32 [4, 8, 4, 2, 64, 64], P('gx', 'gy'), may hold values from -0.706066 to 0.706066, as said below
- pml_flag: int32 [4, 8], P('gx', 'gy'), may hold values 0 or 1
Outputs:
- top_map: float32 [2, 512, 1024], P(None, 'gx', 'gy')
Inputs may be any that keep to these rules, and one draw needn't show every extreme that they name: `coarse_map`: every interface system met in the merges is well conditioned. `fine_maps`: every interface system met in the merges is well conditioned.
All inputs are finite; a program needn't handle non-finite values. No bound on the sum of `pml_flag` on one device may be relied on, other than what follows from the above.
Results may differ from a plain program's by a relative error of at most 0.0003.
Values sent between devices are 32-bit elements; how exact they have to be, the bound alone decides.
A program may use at most 64 MiB of HBM per device.

v0:
```python
import functools
import jax
import jax.numpy as jnp
import numpy as np
from jax import lax
from jax.experimental import pallas as pl
from jax.experimental.pallas import tpu as pltpu
from jax.sharding import PartitionSpec as P

def partner(block, axis, stride):
    count = lax.axis_size(axis)
    route = []
    for low in range(count):
        high = low | 1 << stride
        if high != low and high < count:
            route += [(low, high), (high, low)]
    return lax.ppermute(block, axis, route)


def box_labels(anchor_x, anchor_y, across, upward):
    south = [(0, anchor_y, anchor_x + offset) for offset in range(across)]
    east = [(1, anchor_x + across, anchor_y + offset) for offset in range(upward)]
    north = [(0, anchor_y + upward, anchor_x + offset) for offset in range(across)]
    west = [(1, anchor_x, anchor_y + offset) for offset in range(upward)]
    return south + east + north + west


def pair_tables(former, latter):
    where_latter = {marker: position for position, marker in enumerate(latter)}
    shared = set(former) & set(latter)
    outer_a = [position for position, marker in enumerate(former) if marker not in shared]
    inner_a = [position for position, marker in enumerate(former) if marker in shared]
    inner_b = [where_latter[former[position]] for position in inner_a]
    outer_b = [position for position, marker in enumerate(latter) if marker not in shared]
    joined = [former[position] for position in outer_a] + [latter[position] for position in outer_b]
    tables = (np.array(outer_a), np.array(inner_a), np.array(outer_b), np.array(inner_b))
    return (tables, joined)


def level_tables(points):
    offsets = [(0, points), (points, 0), (0, 2 * points), (2 * points, 0)]

    def labels_at(section, anchor_x, anchor_y):
        if section == 0:
            return box_labels(anchor_x, anchor_y, points, points)
        shift_x, shift_y = offsets[section - 1]
        former = labels_at(section - 1, anchor_x, anchor_y)
        latter = labels_at(section - 1, anchor_x + shift_x, anchor_y + shift_y)
        return pair_tables(former, latter)[1]

    sections = []
    for section in range(1, 5):
        shift_x, shift_y = offsets[section - 1]
        sections.append(
            pair_tables(labels_at(section - 1, 0, 0), labels_at(section - 1, shift_x, shift_y))[0]
        )
    return sections


def fine_tables(points):
    halved = points // 2
    left_tab, left_join = pair_tables(
        box_labels(0, 0, halved, halved), box_labels(0, halved, halved, halved)
    )
    right_tab, right_join = pair_tables(
        box_labels(halved, 0, halved, halved), box_labels(halved, halved, halved, halved)
    )
    whole_tab, whole_join = pair_tables(left_join, right_join)
    where_whole = {marker: position for position, marker in enumerate(whole_join)}
    order = np.array([where_whole[marker] for marker in box_labels(0, 0, points, points)])
    return (left_tab, right_tab, whole_tab, order)


def pick(block, index, axis):
    index = np.asarray(index)
    cuts = [0] + [k for k in range(1, len(index)) if index[k] != index[k - 1] + 1] + [len(index)]
    pieces = []
    for low, high in zip(cuts[:-1], cuts[1:]):
        pieces.append(
            lax.slice_in_dim(block, int(index[low]), int(index[high - 1]) + 1, axis=axis)
        )
    return pieces[0] if len(pieces) == 1 else jnp.concatenate(pieces, axis=axis)


def take(box, rows, cols):
    out = []
    for part in box:
        if rows is not None:
            part = pick(part, rows, 0)
        if cols is not None:
            part = pick(part, cols, 1)
        out.append(part)
    return tuple(out)


def halves(stacked):
    size = stacked.shape[0] // 2
    return stacked[:size], stacked[size:]


def stack(box):
    return jnp.concatenate([box[0], box[1]], axis=0)


def embed(box):
    upper = jnp.concatenate([box[0], -box[1]], axis=1)
    lower = jnp.concatenate([box[1], box[0]], axis=1)
    return jnp.concatenate([upper, lower], axis=0)


def dot(left, right):
    return jnp.dot(left, right, preferred_element_type=jnp.float32)


def split(block):
    high = block.astype(jnp.bfloat16)
    low = (block - high.astype(jnp.float32)).astype(jnp.bfloat16)
    return high, low


def fine_dot(left, right):
    return dot(left[0], right[0]) + (dot(left[0], right[1]) + dot(left[1], right[0]))


def product(left, right):
    return fine_dot(split(embed(left)), split(right))


def unit(size):
    rows = lax.broadcasted_iota(jnp.int32, (2 * size, size), 0)
    cols = lax.broadcasted_iota(jnp.int32, (2 * size, size), 1)
    return jnp.where(rows == cols, 1.0, 0.0).astype(jnp.float32)


def total(block):
    return jnp.sum(jnp.sum(block, axis=0, keepdims=True), axis=1, keepdims=True)[0, 0]


def peak(block):
    return jnp.max(jnp.max(block, axis=0, keepdims=True), axis=1, keepdims=True)[0, 0]


def invert(systems, scratch):
    size = systems[0].shape[1]
    one = unit(size)
    narrow = jnp.bfloat16
    count = len(systems)
    exact = []
    worst = None
    for k, p in enumerate(systems):
        x_ref, r_ref = scratch[k]
        first = one + p
        p_embed = embed(halves(p)).astype(narrow)
        square = dot(p_embed, p.astype(narrow))
        square_embed = embed(halves(square)).astype(narrow)
        second = first + dot(embed(halves(first)).astype(narrow), square.astype(narrow))
        fourth = dot(square_embed, square.astype(narrow))
        x = second + dot(embed(halves(second)).astype(narrow), fourth.astype(narrow))
        a = one - p
        a_split = split(embed(halves(a)))
        r = one - fine_dot(a_split, split(x))
        x_ref[...] = x
        r_ref[...] = r
        norm = total(r * r)
        worst = norm if worst is None else jnp.maximum(worst, norm)
        exact.append((a, a_split))

    def restart():
        norm = jnp.float32(0.0)
        for k in range(count):
            a, a_split = exact[k]
            x_ref, r_ref = scratch[k]
            full = jnp.abs(embed(halves(a)))
            scale = peak(jnp.sum(full, axis=0, keepdims=True)) * peak(
                jnp.sum(full, axis=1, keepdims=True)
            )
            real, imaginary = halves(a)
            x = jnp.concatenate([real.T, -imaginary.T], axis=0) / scale
            r = one - fine_dot(a_split, split(x))
            x_ref[...] = x
            r_ref[...] = r
            norm = jnp.maximum(norm, total(r * r))
        return norm

    worst = lax.cond(worst < 0.25, lambda: worst, restart)

    def unfinished(state):
        return jnp.logical_and(state[0] > 1e-5, state[1] < 200)

    def improve(state):
        norm = jnp.float32(0.0)
        for k in range(count):
            x_ref, r_ref = scratch[k]
            x = x_ref[...]
            x = x + product(halves(x), r_ref[...])
            r = one - fine_dot(exact[k][1], split(x))
            x_ref[...] = x
            r_ref[...] = r
            norm = jnp.maximum(norm, total(r * r))
        return norm, state[1] + 1

    lax.while_loop(unfinished, improve, (worst, jnp.int32(0)))
    return [x_ref[...] + product(halves(x_ref[...]), r_ref[...]) for x_ref, r_ref in scratch[:count]]


def prepare(former, latter, tables):
    outer_a, inner_a, outer_b, inner_b = tables
    size = len(inner_a)
    from_former = take(former, inner_a, np.concatenate([inner_a, outer_a]))
    reflected = product(take(latter, inner_b, inner_b), stack(from_former))
    right_side = jnp.concatenate(
        [reflected[:, size:], -stack(take(latter, inner_b, outer_b))], axis=1
    )
    return reflected[:, :size], right_side


def finish(former, latter, tables, inverse, right_side):
    outer_a, inner_a, outer_b, inner_b = tables
    size_former, size_latter = len(outer_a), len(outer_b)
    solved = product(halves(inverse), right_side)
    rows = np.concatenate([outer_a, inner_a])
    passed = product(take(former, rows, inner_a), solved)
    upper, traces = [], []
    for part, own in zip(halves(passed), take(former, rows, outer_a)):
        wide = jnp.concatenate([own, jnp.zeros((len(rows), size_latter), jnp.float32)], axis=1)
        part = part + wide
        upper.append(part[:size_former])
        traces.append(part[size_former:])
    coupled = product(take(latter, outer_b, inner_b), stack(traces))
    merged = []
    for high, part, own in zip(upper, halves(coupled), take(latter, outer_b, outer_b)):
        wide = jnp.concatenate([jnp.zeros((size_latter, size_former), jnp.float32), own], axis=1)
        merged.append(jnp.concatenate([high, wide - part], axis=0))
    return tuple(merged)


def merge_pair(former, latter, tables, scratch):
    system, right_side = prepare(former, latter, tables)
    (inverse,) = invert([system], [scratch])
    return finish(former, latter, tables, inverse, right_side)


def sides(own_ref, partner_ref, swapped):
    former, latter = [], []
    for part in range(2):
        own, other = own_ref[part], partner_ref[part]
        former.append(jnp.where(swapped, other, own))
        latter.append(jnp.where(swapped, own, other))
    return tuple(former), tuple(latter)


def box_kernel(fine_set, flag_ref, coarse_ref, fine_ref, out_ref, *scratch):
    left_tab, right_tab, whole_tab, order = fine_set
    pairs = [scratch[0:2], scratch[2:4], scratch[4:6]]

    @pl.when(flag_ref[0, 0] > 0)
    def _():
        pieces = [(fine_ref[k, 0], fine_ref[k, 1]) for k in range(4)]
        left_system, left_side = prepare(pieces[0], pieces[1], left_tab)
        right_system, right_side = prepare(pieces[2], pieces[3], right_tab)
        left_inverse, right_inverse = invert([left_system, right_system], pairs)
        left_map = finish(pieces[0], pieces[1], left_tab, left_inverse, left_side)
        right_map = finish(pieces[2], pieces[3], right_tab, right_inverse, right_side)
        whole = take(merge_pair(left_map, right_map, whole_tab, pairs[2]), order, order)
        out_ref[0] = whole[0]
        out_ref[1] = whole[1]

    @pl.when(flag_ref[0, 0] <= 0)
    def _():
        out_ref[...] = coarse_ref[...]


def pair_kernel(tables, place_ref, own_ref, partner_ref, out_ref, *scratch):
    former, latter = sides(own_ref, partner_ref, place_ref[0] > 0)
    merged = merge_pair(former, latter, tables, scratch)
    out_ref[0] = merged[0]
    out_ref[1] = merged[1]


def half_kernel(tables, next_tables, place_ref, own_ref, partner_ref, send_ref, inner_ref, rows_ref, work_ref, *scratch):
    former, latter = sides(own_ref, partner_ref, place_ref[0] > 0)
    merged = merge_pair(former, latter, tables, scratch)
    outer_a, inner_a, outer_b, inner_b = next_tables
    latter_side = place_ref[1] > 0
    size = len(inner_a)
    tile = rows_ref.shape[1]
    near = np.concatenate([inner_a, outer_a])
    far = np.concatenate([inner_b, outer_b])
    for part in range(2):
        chosen = jnp.where(
            latter_side,
            pick(pick(merged[part], far, 0), far, 1),
            pick(pick(merged[part], near, 0), near, 1),
        )
        inner_ref[part] = chosen[:size]
        work_ref[part] = chosen[size:]
        rows_ref[part] = work_ref[part, pl.ds(pl.multiple_of(place_ref[2] * tile, tile), tile), :]
        send_ref[part, :, :size] = chosen[:size, :size]
        send_ref[part, :, size:] = inner_ref[
            part, :, pl.ds(pl.multiple_of(size + place_ref[3] * tile, 128), tile)
        ]


def tile_kernel(place_ref, inner_ref, received_ref, rows_ref, out_ref, *scratch):
    latter_side = place_ref[1] > 0
    latter_tile = place_ref[4] > 0
    size = inner_ref.shape[1]
    tile = rows_ref.shape[1]
    columns = pl.ds(pl.multiple_of(size + place_ref[3] * tile, 128), tile)
    own_inner = [inner_ref[part, :, :size] for part in range(2)]
    got_inner = [received_ref[part, :, :size] for part in range(2)]
    former = [jnp.where(latter_side, got_inner[k], own_inner[k]) for k in range(2)]
    latter = [jnp.where(latter_side, own_inner[k], got_inner[k]) for k in range(2)]
    same = latter_side == latter_tile
    outward = [
        jnp.where(same, inner_ref[k, :, columns], received_ref[k, :, size:]) for k in range(2)
    ]
    reflected = product(latter, jnp.concatenate([stack(former), stack(outward)], axis=1))
    (inverse,) = invert([reflected[:, :size]], [scratch])
    right_side = jnp.where(latter_tile, -stack(outward), reflected[:, size:])
    solved = product(halves(inverse), right_side)
    traces = product(former, solved) + jnp.where(latter_tile, 0.0, stack(outward))
    applied = jnp.where(latter_side, -traces, solved)
    coupling = [rows_ref[k, :, :size] for k in range(2)]
    through = halves(product(coupling, applied))
    for k in range(2):
        out_ref[k] = through[k] + jnp.where(same, rows_ref[k, :, columns], 0.0)


def work(*sizes):
    return [pltpu.VMEM((2 * size, size), jnp.float32) for size in sizes for _ in range(2)]


def call(kernel, shapes, scratch, place, *blocks):
    vmem = pl.BlockSpec(memory_space=pltpu.VMEM)
    outs = [jax.ShapeDtypeStruct(shape, jnp.float32) for shape in shapes]
    single = len(outs) == 1
    return pl.pallas_call(
        kernel,
        out_shape=outs[0] if single else tuple(outs),
        in_specs=[pl.BlockSpec(memory_space=pltpu.SMEM)] + [vmem] * len(blocks),
        out_specs=vmem if single else tuple([vmem] * len(outs)),
        scratch_shapes=scratch,
        compiler_params=pltpu.CompilerParams(vmem_limit_bytes=48 * 1024 * 1024),
    )(place, *blocks)


def body(coarse_map, fine_maps, pml_flag):
    points = coarse_map.shape[-1] // 4
    fine_set = fine_tables(points)
    sections = level_tables(points)
    inner = [len(section[1]) for section in sections]
    width = [len(section[0]) + len(section[2]) for section in sections]
    tile = 4 * points
    gx_index = lax.axis_index("gx")
    gy_index = lax.axis_index("gy")

    def place(swapped):
        return jnp.stack(
            [
                swapped,
                gx_index // 2 % 2,
                gx_index % 2,
                gy_index % 2,
                gy_index // 2 % 2,
            ]
        ).astype(jnp.int32)

    boxed = call(
        functools.partial(box_kernel, fine_set),
        [coarse_map.shape[2:]],
        work(points // 2, points // 2, points),
        pml_flag,
        coarse_map[0, 0],
        fine_maps[0, 0],
    )
    one = call(
        functools.partial(pair_kernel, sections[0]),
        [(2, width[0], width[0])],
        work(inner[0]),
        place(gy_index % 2),
        boxed,
        partner(boxed, "gy", 0),
    )
    two = call(
        functools.partial(pair_kernel, sections[1]),
        [(2, width[1], width[1])],
        work(inner[1]),
        place(gx_index % 2),
        one,
        partner(one, "gx", 0),
    )
    sent, own_inner, own_rows = call(
        functools.partial(half_kernel, sections[2], sections[3]),
        [(2, inner[3], inner[3] + tile), (2, inner[3], width[2]), (2, tile, width[2])],
        [pltpu.VMEM((2, width[2] - inner[3], width[2]), jnp.float32)] + work(inner[2]),
        place(gy_index // 2 % 2),
        two,
        partner(two, "gy", 1),
    )
    return call(
        tile_kernel,
        [(2, tile, tile)],
        work(inner[3]),
        place(gx_index // 2 % 2),
        own_inner,
        partner(sent, "gx", 1),
        own_rows,
    )


def solution(mesh):
    placed = (P("gx", "gy", None, None, None), P("gx", "gy", None, None, None, None), P("gx", "gy"))
    return jax.shard_map(
        body, mesh=mesh, in_specs=placed, out_specs=P(None, "gx", "gy"), check_vma=False
    )
```

profile of v0, /device:TPU:0, one launch (start us, length us, event | category | flops | bytes accessed | tf_op | source)
XLA Modules:
  0.0 63.8 jit_solution(400386764593872730)
XLA Ops:
  0.7 0.0 copy-start
  0.7 0.9 %copy-done = f32[1,1,4,2,64,64]{5,4,3,2,1,0:T(8,128)S(1)} copy-done((f32[1,1,4,2,64,64]{5,4,3,2,1,0:T(8,128)S(1)}, f32[1,1,4,2,64,64]{5,4,3,2,1,0:T(8,128)}, u32[]{:S(2)}) %copy-start) | copy-done | bytes 131096
  1.6 0.0 copy-start.1
  1.6 0.9 %copy-done.1 = f32[1,1,2,128,128]{4,3,2,1,0:T(8,128)S(1)} copy-done((f32[1,1,2,128,128]{4,3,2,1,0:T(8,128)S(1)}, f32[1,1,2,128,128]{4,3,2,1,0:T(8,128)}, u32[]{:S(2)}) %copy-start.1) | copy-done | bytes 131096
  2.5 0.6 collective-permute-start
  3.1 0.1 stack.23.place_ref
  3.2 0.9 %collective-permute-done.partner_ref = f32[2,128,128]{2,1,0:T(8,128)S(1)} collective-permute-done((f32[2,128,128]{2,1,0:T(8,128)S(1)}, f32[2,128,128]{2,1,0:T(8,128)S(1)}, u32[]{:S(2)}, u32[]{:S(2)}) %collective-permute-start) | collective-permute-done | bytes 131104 | tf_op jit(solution)/shard_map/ppermute | solution.py:17
  4.1 3.1 %shard_map.38.own_ref = f32[2,192,192]{2,1,0:T(8,128)S(1)} custom-call(s32[5]{0:T(128)S(1)} %stack.23.place_ref, f32[2,128,128]{2,1,0:T(8,128)S(1)} %shard_map.37.own_ref, f32[2,128,128]{2,1,0:T(8,128)S(1)} %collective-permute-done.partner_ref), custom_call_target="tpu_custom_call" | custom-call | tf_op jit(solution)/shard_map/pallas_call | solution.py:338
  7.1 8.3 %collective-permute-start.1 = (f32[2,192,192]{2,1,0:T(8,128)S(1)}, f32[2,192,192]{2,1,0:T(8,128)S(1)}, u32[]{:S(2)}, u32[]{:S(2)}) collective-permute-start(f32[2,192,192]{2,1,0:T(8,128)S(1)} %shard_map.38.own_ref), channel_id=1, source_target_pairs={{0,8},{8,0},{16,24},{24,16},{1,9},{9,1},{17,25},{25,17},{2,10},{10... | collective-permute-start | bytes 884744 | tf_op jit(solution)/shard_map/ppermute | solution.py:17
  15.4 0.1 stack.22.place_ref
  15.5 9.3 %collective-permute-done.1.partner_ref = f32[2,192,192]{2,1,0:T(8,128)S(1)} collective-permute-done((f32[2,192,192]{2,1,0:T(8,128)S(1)}, f32[2,192,192]{2,1,0:T(8,128)S(1)}, u32[]{:S(2)}, u32[]{:S(2)}) %collective-permute-start.1) | collective-permute-done | bytes 294944 | tf_op jit(solution)/shard_map/ppermute | solution.py:17
  24.9 3.5 %shard_map.39.own_ref = f32[2,256,256]{2,1,0:T(8,128)S(1)} custom-call(s32[5]{0:T(128)S(1)} %stack.22.place_ref, f32[2,192,192]{2,1,0:T(8,128)S(1)} %shard_map.38.own_ref, f32[2,192,192]{2,1,0:T(8,128)S(1)} %collective-permute-done.1.partner_ref), custom_call_target="tpu_custom_call" | custom-call | tf_op jit(solution)/shard_map/pallas_call | solution.py:338
  28.4 0.1 collective-permute-start.2
  28.5 0.1 stack.21.place_ref
  28.6 13.3 %collective-permute-done.2.partner_ref = f32[2,256,256]{2,1,0:T(8,128)S(1)} collective-permute-done((f32[2,256,256]{2,1,0:T(8,128)S(1)}, f32[2,256,256]{2,1,0:T(8,128)S(1)}, u32[]{:S(2)}, u32[]{:S(2)}) %collective-permute-start.2) | collective-permute-done | bytes 524320 | tf_op jit(solution)/shard_map/ppermute | solution.py:17
  41.9 4.1 %shard_map.40 = (f32[2,128,256]{2,1,0:T(8,128)S(1)}, f32[2,128,384]{2,1,0:T(8,128)S(1)}, f32[2,128,384]{2,1,0:T(8,128)S(1)}) custom-call(s32[5]{0:T(128)S(1)} %stack.21.place_ref, f32[2,256,256]{2,1,0:T(8,128)S(1)} %shard_map.39.own_ref, f32[2,256,256]{2,1,0:T(8,128)S(1)} %collective-permute-done.2.partner_ref), custom_call_target="tpu_custom_call" | custom-call | tf_op jit(solution)/shard_map/pallas_call | solution.py:338
  45.9 2.5 %collective-permute-start.3 = (f32[2,128,256]{2,1,0:T(8,128)S(1)}, f32[2,128,256]{2,1,0:T(8,128)S(1)}, u32[]{:S(2)}, u32[]{:S(2)}) collective-permute-start(f32[2,128,256]{2,1,0:T(8,128)S(1)} %get-tuple-element.9), channel_id=1, source_target_pairs={{0,16},{16,0},{8,24},{24,8},{1,17},{17,1},{9,25},{25,9},{2,18},{18... | collective-permute-start | bytes 786440 | tf_op jit(solution)/shard_map/ppermute | solution.py:17
  48.5 0.1 stack.20.place_ref
  48.6 10.9 %collective-permute-done.3.received_ref = f32[2,128,256]{2,1,0:T(8,128)S(1)} collective-permute-done((f32[2,128,256]{2,1,0:T(8,128)S(1)}, f32[2,128,256]{2,1,0:T(8,128)S(1)}, u32[]{:S(2)}, u32[]{:S(2)}) %collective-permute-start.3) | collective-permute-done | bytes 262176 | tf_op jit(solution)/shard_map/ppermute | solution.py:17
  59.5 4.3 %shard_map.41 = f32[2,128,128]{2,1,0:T(8,128)} custom-call(s32[5]{0:T(128)S(1)} %stack.20.place_ref, f32[2,128,384]{2,1,0:T(8,128)S(1)} %get-tuple-element.8.inner_ref, f32[2,128,256]{2,1,0:T(8,128)S(1)} %collective-permute-done.3.received_ref, f32[2,128,384]{2,1,0:T(8,128)S(1)} %get-tuple-element.10.rows_ref), custom_call_target="tpu_custom_call" | custom-call | tf_op jit(solution)/shard_map/pallas_call | solution.py:338
  (1 shorter events, 0.0 us)
Async XLA Ops:
  0.7 1.0 %copy-start = (f32[1,1,4,2,64,64]{5,4,3,2,1,0:T(8,128)S(1)}, f32[1,1,4,2,64,64]{5,4,3,2,1,0:T(8,128)}, u32[]{:S(2)}) copy-start(f32[1,1,4,2,64,64]{5,4,3,2,1,0:T(8,128)} %param.4) | copy-start | bytes 393220
  1.6 0.9 %copy-start.1 = (f32[1,1,2,128,128]{4,3,2,1,0:T(8,128)S(1)}, f32[1,1,2,128,128]{4,3,2,1,0:T(8,128)}, u32[]{:S(2)}) copy-start(f32[1,1,2,128,128]{4,3,2,1,0:T(8,128)} %param.3) | copy-start | bytes 393220
  2.5 1.5 %collective-permute-start = (f32[2,128,128]{2,1,0:T(8,128)S(1)}, f32[2,128,128]{2,1,0:T(8,128)S(1)}, u32[]{:S(2)}, u32[]{:S(2)}) collective-permute-start(f32[2,128,128]{2,1,0:T(8,128)S(1)} %shard_map.37.own_ref), channel_id=1, source_target_pairs={{0,1},{1,0},{2,3},{3,2},{4,5},{5,4},{6,7},{7,6},{8,9},{9,8},{10,11... | collective-permute-start | bytes 393224 | tf_op jit(solution)/shard_map/ppermute | solution.py:17
  7.1 17.7 %collective-permute-start.1 = (f32[2,192,192]{2,1,0:T(8,128)S(1)}, f32[2,192,192]{2,1,0:T(8,128)S(1)}, u32[]{:S(2)}, u32[]{:S(2)}) collective-permute-start(f32[2,192,192]{2,1,0:T(8,128)S(1)} %shard_map.38.own_ref), channel_id=1, source_target_pairs={{0,8},{8,0},{16,24},{24,16},{1,9},{9,1},{17,25},{25,17},{2,10},{10... | collective-permute-start | bytes 884744 | tf_op jit(solution)/shard_map/ppermute | solution.py:17
  28.4 13.5 %collective-permute-start.2 = (f32[2,256,256]{2,1,0:T(8,128)S(1)}, f32[2,256,256]{2,1,0:T(8,128)S(1)}, u32[]{:S(2)}, u32[]{:S(2)}) collective-permute-start(f32[2,256,256]{2,1,0:T(8,128)S(1)} %shard_map.39.own_ref), channel_id=1, source_target_pairs={{0,2},{2,0},{1,3},{3,1},{4,6},{6,4},{5,7},{7,5},{8,10},{10,8},{9,1... | collective-permute-start | bytes 1572872 | tf_op jit(solution)/shard_map/ppermute | solution.py:17
  45.9 13.5 %collective-permute-start.3 = (f32[2,128,256]{2,1,0:T(8,128)S(1)}, f32[2,128,256]{2,1,0:T(8,128)S(1)}, u32[]{:S(2)}, u32[]{:S(2)}) collective-permute-start(f32[2,128,256]{2,1,0:T(8,128)S(1)} %get-tuple-element.9), channel_id=1, source_target_pairs={{0,16},{16,0},{8,24},{24,8},{1,17},{17,1},{9,25},{25,9},{2,18},{18... | collective-permute-start | bytes 786440 | tf_op jit(solution)/shard_map/ppermute | solution.py:17
where the time goes:
time: 63.8 us
  waiting for transfers between devices  34.4 us (54%)
  Pallas kernels  15 us (24%)
  starting transfers between devices  11.5 us (18%)
  local copies, waits for them, and re-layouts  2.19 us (3%)
  between operations  0.7 us (1%)
    ppermute x4, waiting for transfers between devices, partner(): return lax.ppermute(block, axis, route)  34.4 us
    pallas_call x5, Pallas kernels, call(): pl.pallas_call(kernel, out_shape=outs[0] if single else tuple(outs), in_s...  15 us
    ppermute x4, starting transfers between devices, partner(): return lax.ppermute(block, axis, route)  11.5 us
    unnamed x4, local copies, waits for them, and re-layouts  1.85 us
  transfers between devices with their start and end apart: 4, of which 4 were waited for; matrix products, arithmetic and copies ran while one was open for 1% of the time, Pallas kernels for 0%

commit v1 on v0

--- a/solution.py
+++ b/solution.py
@@ -277,11 +277,13 @@
     out_ref[1] = merged[1]
 
 
-def half_kernel(tables, next_tables, place_ref, own_ref, partner_ref, send_ref, inner_ref, rows_ref, work_ref, *scratch):
+def half_kernel(tables, next_tables, place_ref, own_ref, partner_ref, face_ref, outward_ref, rows_ref, *scratch):
     former, latter = sides(own_ref, partner_ref, place_ref[0] > 0)
     merged = merge_pair(former, latter, tables, scratch)
     outer_a, inner_a, outer_b, inner_b = next_tables
     latter_side = place_ref[1] > 0
+    second_rows = place_ref[2] > 0
+    second_cols = place_ref[3] > 0
     size = len(inner_a)
     tile = rows_ref.shape[1]
     near = np.concatenate([inner_a, outer_a])
@@ -292,39 +294,182 @@
             pick(pick(merged[part], far, 0), far, 1),
             pick(pick(merged[part], near, 0), near, 1),
         )
-        inner_ref[part] = chosen[:size]
-        work_ref[part] = chosen[size:]
-        rows_ref[part] = work_ref[part, pl.ds(pl.multiple_of(place_ref[2] * tile, tile), tile), :]
-        send_ref[part, :, :size] = chosen[:size, :size]
-        send_ref[part, :, size:] = inner_ref[
-            part, :, pl.ds(pl.multiple_of(size + place_ref[3] * tile, 128), tile)
-        ]
-
-
-def tile_kernel(place_ref, inner_ref, received_ref, rows_ref, out_ref, *scratch):
+        low, high = size + tile, size + 2 * tile
+        cols = jnp.where(second_cols, chosen[:, low:high], chosen[:, size:low])
+        face_ref[part] = chosen[:size, :size]
+        outward_ref[part] = cols[:size]
+        coupling = chosen[:, :size]
+        rows_ref[part, :, :size] = jnp.where(second_rows, coupling[low:high], coupling[size:low])
+        rows_ref[part, :, size:] = jnp.where(second_rows, cols[low:high], cols[size:low])
+
+
+def tile_kernel(place_ref, face_ref, outward_ref, got_face_ref, got_outward_ref, rows_ref, out_ref, *scratch):
     latter_side = place_ref[1] > 0
     latter_tile = place_ref[4] > 0
-    size = inner_ref.shape[1]
-    tile = rows_ref.shape[1]
-    columns = pl.ds(pl.multiple_of(size + place_ref[3] * tile, 128), tile)
-    own_inner = [inner_ref[part, :, :size] for part in range(2)]
-    got_inner = [received_ref[part, :, :size] for part in range(2)]
-    former = [jnp.where(latter_side, got_inner[k], own_inner[k]) for k in range(2)]
-    latter = [jnp.where(latter_side, own_inner[k], got_inner[k]) for k in range(2)]
+    size = face_ref.shape[1]
+    former = [jnp.where(latter_side, got_face_ref[k], face_ref[k]) for k in range(2)]
+    latter = [jnp.where(latter_side, face_ref[k], got_face_ref[k]) for k in range(2)]
     same = latter_side == latter_tile
-    outward = [
-        jnp.where(same, inner_ref[k, :, columns], received_ref[k, :, size:]) for k in range(2)
-    ]
-    reflected = product(latter, jnp.concatenate([stack(former), stack(outward)], axis=1))
+    outward = stack([jnp.where(same, outward_ref[k], got_outward_ref[k]) for k in range(2)])
+    reflected = product(latter, jnp.concatenate([stack(former), outward], axis=1))
     (inverse,) = invert([reflected[:, :size]], [scratch])
-    right_side = jnp.where(latter_tile, -stack(outward), reflected[:, size:])
+    right_side = jnp.where(latter_tile, -outward, reflected[:, size:])
     solved = product(halves(inverse), right_side)
-    traces = product(former, solved) + jnp.where(latter_tile, 0.0, stack(outward))
+    traces = product(former, solved) + jnp.where(latter_tile, 0.0, outward)
     applied = jnp.where(latter_side, -traces, solved)
     coupling = [rows_ref[k, :, :size] for k in range(2)]
     through = halves(product(coupling, applied))
     for k in range(2):
-        out_ref[k] = through[k] + jnp.where(same, rows_ref[k, :, columns], 0.0)
+        out_ref[k] = through[k] + jnp.where(same, rows_ref[k, :, size:], 0.0)
+
+
+def flipped(index, bit):
+    step = 2**bit
+    return index + step * (1 - 2 * lax.rem(lax.div(index, step), 2))
+
+
+def hop(source, target, sems, slot, device):
+    return pltpu.make_async_remote_copy(
+        src_ref=source,
+        dst_ref=target,
+        send_sem=sems[0].at[slot],
+        recv_sem=sems[1].at[slot],
+        device_id=device,
+        device_id_type=pl.DeviceIdType.MESH,
+    )
+
+
+def greet(devices):
+    barrier = pltpu.get_barrier_semaphore()
+    for device in devices:
+        pl.semaphore_signal(
+            barrier, inc=1, device_id=device, device_id_type=pl.DeviceIdType.MESH
+        )
+    pl.semaphore_wait(barrier, len(devices))
+
+
+def swap_kernel(axis, bit, chunks, own_ref, out_ref, far_send, far_recv, near_send, near_recv):
+    gx, gy = lax.axis_index("gx"), lax.axis_index("gy")
+    peer = (flipped(gx, bit), gy) if axis == "gx" else (gx, flipped(gy, bit))
+    sibling = (gx, flipped(gy, 0))
+    mine = lax.rem(gy, 2)
+    greet([peer, sibling])
+    rows = own_ref.shape[1] // chunks
+    far, near = (far_send, far_recv), (near_send, near_recv)
+    out, relays = [], []
+    for k in range(chunks):
+        spot = (mine, pl.ds(k * rows, rows))
+        copy = hop(own_ref.at[spot], out_ref.at[spot], far, k, peer)
+        copy.start()
+        out.append(copy)
+        relays.append(hop(out_ref.at[spot], out_ref.at[spot], near, k, sibling))
+    for k in range(chunks):
+        out[k].wait_recv()
+        relays[k].start()
+    for k in range(chunks):
+        relays[k].wait_recv()
+    for k in range(chunks):
+        out[k].wait_send()
+        relays[k].wait_send()
+
+
+def line_kernel(face_ref, outward_ref, got_face_ref, got_outward_ref, far_send, far_recv, on_send, on_recv, near_send, near_recv):
+    gx, gy = lax.axis_index("gx"), lax.axis_index("gy")
+    low, second = lax.rem(gx, 2), lax.rem(lax.div(gx, 2), 2)
+    middle = low != second
+    across = (gx + 1 - 2 * second, gy)
+    along = (flipped(gx, 0), gy)
+    sibling = (gx, flipped(gy, 0))
+    mine = lax.rem(gy, 2)
+    group = lax.rem(lax.div(gy, 2), 2)
+    gives = group == second
+    takes = group != second
+
+    @pl.when(middle)
+    def _():
+        greet([across, along, sibling])
+
+    @pl.when(jnp.logical_not(middle))
+    def _():
+        greet([along, sibling])
+
+    rows = outward_ref.shape[1] // 2
+    spots = [(part, pl.ds(k * rows, rows)) for part in range(2) for k in range(2)]
+    far, on, near = (far_send, far_recv), (on_send, on_recv), (near_send, near_recv)
+    face_far = hop(face_ref.at[mine], got_face_ref.at[mine], far, 0, across)
+    face_on = hop(got_face_ref.at[mine], got_face_ref.at[mine], on, 0, along)
+    face_near = hop(got_face_ref.at[mine], got_face_ref.at[mine], near, 0, sibling)
+    cols_far = [
+        hop(outward_ref.at[spot], got_outward_ref.at[spot], far, k + 1, across)
+        for k, spot in enumerate(spots)
+    ]
+    cols_on = [
+        hop(got_outward_ref.at[spot], got_outward_ref.at[spot], on, k + 1, along)
+        for k, spot in enumerate(spots)
+    ]
+
+    @pl.when(middle)
+    def _():
+        face_far.start()
+
+        @pl.when(gives)
+        def _():
+            for copy in cols_far:
+                copy.start()
+
+        face_far.wait_recv()
+        face_on.start()
+        face_near.start()
+
+        @pl.when(takes)
+        def _():
+            for first, then in zip(cols_far, cols_on):
+                first.wait_recv()
+                then.start()
+            for then in cols_on:
+                then.wait_send()
+
+        @pl.when(gives)
+        def _():
+            for copy in cols_far:
+                copy.wait_send()
+
+        face_far.wait_send()
+        face_on.wait_send()
+
+    @pl.when(jnp.logical_not(middle))
+    def _():
+        face_on.wait_recv()
+        face_near.start()
+
+        @pl.when(takes)
+        def _():
+            for copy in cols_on:
+                copy.wait_recv()
+
+    face_near.wait_recv()
+    face_near.wait_send()
+
+
+def exchange(kernel, identity, copies, *blocks):
+    vmem = pl.BlockSpec(memory_space=pltpu.VMEM)
+    outs = [jax.ShapeDtypeStruct(block.shape, block.dtype) for block in blocks]
+    single = len(outs) == 1
+    return pl.pallas_call(
+        kernel,
+        out_shape=outs[0] if single else tuple(outs),
+        in_specs=[vmem] * len(blocks),
+        out_specs=vmem if single else tuple([vmem] * len(outs)),
+        scratch_shapes=[pltpu.SemaphoreType.DMA((count,)) for count in copies for _ in range(2)],
+        compiler_params=pltpu.CompilerParams(collective_id=identity, has_side_effects=True),
+    )(*blocks)
+
+
+def swap(block, axis, bit, identity):
+    chunks = 4
+    return exchange(
+        functools.partial(swap_kernel, axis, bit, chunks), identity, (chunks, chunks), block
+    )
 
 
 def work(*sizes):
@@ -388,23 +533,26 @@
         work(inner[1]),
         place(gx_index % 2),
         one,
-        partner(one, "gx", 0),
-    )
-    sent, own_inner, own_rows = call(
+        swap(one, "gx", 0, 0),
+    )
+    face, outward, own_rows = call(
         functools.partial(half_kernel, sections[2], sections[3]),
-        [(2, inner[3], inner[3] + tile), (2, inner[3], width[2]), (2, tile, width[2])],
-        [pltpu.VMEM((2, width[2] - inner[3], width[2]), jnp.float32)] + work(inner[2]),
+        [(2, inner[3], inner[3]), (2, inner[3], tile), (2, tile, inner[3] + tile)],
+        work(inner[2]),
         place(gy_index // 2 % 2),
         two,
-        partner(two, "gy", 1),
-    )
+        swap(two, "gy", 1, 1),
+    )
+    got_face, got_outward = exchange(line_kernel, 2, (5, 5, 1), face, outward)
     return call(
         tile_kernel,
         [(2, tile, tile)],
         work(inner[3]),
         place(gx_index // 2 % 2),
-        own_inner,
-        partner(sent, "gx", 1),
+        face,
+        outward,
+        got_face,
+        got_outward,
         own_rows,
     )
 

time: 63.8 us -> 68.2 us (1.069)
  the two profiles are of different devices: /device:TPU:0 before, /device:TPU:6 now
where the time goes in v1:
time: 68.2 us; the launch traced here: 67.8 us
  Pallas kernels  55 us (81%)
  local copies, waits for them, and re-layouts  10.9 us (16%)
  waiting for transfers between devices  0.93 us (1%)
  between operations  0.86 us (1%)
    pallas_call x3, Pallas kernels, exchange(): pl.pallas_call(kernel, out_shape=outs[0] if single else tuple(outs), in_s...  40.1 us
    pallas_call x5, Pallas kernels, call(): pl.pallas_call(kernel, out_shape=outs[0] if single else tuple(outs), in_s...  14.9 us
    unnamed x28, local copies, waits for them, and re-layouts  10.6 us
  transfers between devices with their start and end apart: 1, of which 1 were waited for; matrix products, arithmetic and copies ran while one was open for 0% of the time, Pallas kernels for 0%

profile of v1, /device:TPU:6, one launch (start us, length us, event | category | flops | bytes accessed | tf_op | source)
XLA Modules:
  0.0 67.8 jit_solution(10904765139769860701)
XLA Ops:
  0.7 0.0 copy-start.10
  0.7 0.9 %copy-done.10 = f32[1,1,4,2,64,64]{5,4,3,2,1,0:T(8,128)S(1)} copy-done((f32[1,1,4,2,64,64]{5,4,3,2,1,0:T(8,128)S(1)}, f32[1,1,4,2,64,64]{5,4,3,2,1,0:T(8,128)}, u32[]{:S(2)}) %copy-start.10) | copy-done | bytes 131096
  1.6 0.0 copy-start.11
  1.6 0.9 %copy-done.11 = f32[1,1,2,128,128]{4,3,2,1,0:T(8,128)S(1)} copy-done((f32[1,1,2,128,128]{4,3,2,1,0:T(8,128)S(1)}, f32[1,1,2,128,128]{4,3,2,1,0:T(8,128)}, u32[]{:S(2)}) %copy-start.11) | copy-done | bytes 131096
  2.5 0.1 collective-permute-start
  2.7 0.1 stack.23.place_ref
  2.8 0.1 stack.22.place_ref
  2.8 0.1 stack.21.place_ref
  2.9 0.1 stack.20.place_ref
  3.0 0.9 %collective-permute-done.partner_ref = f32[2,128,128]{2,1,0:T(8,128)S(1)} collective-permute-done((f32[2,128,128]{2,1,0:T(8,128)S(1)}, f32[2,128,128]{2,1,0:T(8,128)S(1)}, u32[]{:S(2)}, u32[]{:S(2)}) %collective-permute-start) | collective-permute-done | bytes 131104 | tf_op jit(solution)/shard_map/ppermute | solution.py:17
  3.9 3.1 %shard_map.38.own_ref = f32[2,192,192]{2,1,0:T(8,128)S(1)} custom-call(s32[5]{0:T(128)S(1)} %stack.23.place_ref, f32[2,128,128]{2,1,0:T(8,128)S(1)} %shard_map.37.own_ref, f32[2,128,128]{2,1,0:T(8,128)S(1)} %collective-permute-done.partner_ref), custom_call_target="tpu_custom_call" | custom-call | tf_op jit(solution)/shard_map/pallas_call | solution.py:483
  7.0 0.0 copy-start.2
  7.0 0.7 %copy-done.2 = f32[2,192,192]{2,1,0:T(8,128)} copy-done((f32[2,192,192]{2,1,0:T(8,128)}, f32[2,192,192]{2,1,0:T(8,128)S(1)}, u32[]{:S(2)}) %copy-start.2) | copy-done | bytes 294936
  7.8 14.7 %shard_map.39.partner_ref = f32[2,192,192]{2,1,0:T(8,128)} custom-call(f32[2,192,192]{2,1,0:T(8,128)} %copy-done.2), custom_call_target="tpu_custom_call" | custom-call | tf_op jit(solution)/shard_map/pallas_call | solution.py:458
  22.5 0.0 copy-start.3
  22.5 1.0 %copy-done.3 = f32[2,192,192]{2,1,0:T(8,128)S(1)} copy-done((f32[2,192,192]{2,1,0:T(8,128)S(1)}, f32[2,192,192]{2,1,0:T(8,128)}, u32[]{:S(2)}) %copy-start.3) | copy-done | bytes 294936
  23.5 0.0 copy-start.5
  23.5 1.0 %copy-done.5 = f32[2,192,192]{2,1,0:T(8,128)S(1)} copy-done((f32[2,192,192]{2,1,0:T(8,128)S(1)}, f32[2,192,192]{2,1,0:T(8,128)}, u32[]{:S(2)}) %copy-start.5) | copy-done | bytes 294936
  24.5 3.5 %shard_map.40.own_ref = f32[2,256,256]{2,1,0:T(8,128)S(1)} custom-call(s32[5]{0:T(128)S(1)} %stack.22.place_ref, f32[2,192,192]{2,1,0:T(8,128)S(1)} %copy-done.3, f32[2,192,192]{2,1,0:T(8,128)S(1)} %copy-done.5), custom_call_target="tpu_custom_call" | custom-call | tf_op jit(solution)/shard_map/pallas_call | solution.py:483
  28.0 0.0 copy-start
  28.0 0.8 %copy-done = f32[2,256,256]{2,1,0:T(8,128)} copy-done((f32[2,256,256]{2,1,0:T(8,128)}, f32[2,256,256]{2,1,0:T(8,128)S(1)}, u32[]{:S(2)}) %copy-start) | copy-done | bytes 524312
  28.8 11.5 %shard_map.41.partner_ref = f32[2,256,256]{2,1,0:T(8,128)} custom-call(f32[2,256,256]{2,1,0:T(8,128)} %copy-done), custom_call_target="tpu_custom_call" | custom-call | tf_op jit(solution)/shard_map/pallas_call | solution.py:458
  40.3 0.0 copy-start.1
  40.3 1.0 %copy-done.1 = f32[2,256,256]{2,1,0:T(8,128)S(1)} copy-done((f32[2,256,256]{2,1,0:T(8,128)S(1)}, f32[2,256,256]{2,1,0:T(8,128)}, u32[]{:S(2)}) %copy-start.1) | copy-done | bytes 524312
  41.3 0.0 copy-start.4
  41.3 1.0 %copy-done.4 = f32[2,256,256]{2,1,0:T(8,128)S(1)} copy-done((f32[2,256,256]{2,1,0:T(8,128)S(1)}, f32[2,256,256]{2,1,0:T(8,128)}, u32[]{:S(2)}) %copy-start.4) | copy-done | bytes 524312
  42.3 4.0 %shard_map.42 = (f32[2,128,128]{2,1,0:T(8,128)S(1)}, f32[2,128,128]{2,1,0:T(8,128)S(1)}, f32[2,128,256]{2,1,0:T(8,128)S(1)}) custom-call(s32[5]{0:T(128)S(1)} %stack.21.place_ref, f32[2,256,256]{2,1,0:T(8,128)S(1)} %copy-done.1, f32[2,256,256]{2,1,0:T(8,128)S(1)} %copy-done.4), custom_call_target="tpu_custom_call" | custom-call | tf_op jit(solution)/shard_map/pallas_call | solution.py:483
  46.4 0.0 copy-start.6
  46.4 0.6 copy-done.6
  47.0 0.0 copy-start.8
  47.0 0.7 copy-done.8
  47.7 0.0 copy-start.7
  47.7 0.0 copy-start.9
  47.7 14.0 %shard_map.43 = (f32[2,128,128]{2,1,0:T(8,128)}, f32[2,128,128]{2,1,0:T(8,128)}) custom-call(f32[2,128,128]{2,1,0:T(8,128)} %copy-done.6, f32[2,128,128]{2,1,0:T(8,128)} %copy-done.8), custom_call_target="tpu_custom_call" | custom-call | tf_op jit(solution)/shard_map/pallas_call | solution.py:458
  61.7 0.0 copy-done.7
  61.7 0.0 copy-done.9
  61.7 0.0 copy-start.12
  61.7 0.9 %copy-done.12 = f32[2,128,128]{2,1,0:T(8,128)S(1)} copy-done((f32[2,128,128]{2,1,0:T(8,128)S(1)}, f32[2,128,128]{2,1,0:T(8,128)}, u32[]{:S(2)}) %copy-start.12) | copy-done | bytes 131096
  62.6 0.0 copy-start.13
  62.6 0.9 %copy-done.13 = f32[2,128,128]{2,1,0:T(8,128)S(1)} copy-done((f32[2,128,128]{2,1,0:T(8,128)S(1)}, f32[2,128,128]{2,1,0:T(8,128)}, u32[]{:S(2)}) %copy-start.13) | copy-done | bytes 131096
  63.5 4.3 %shard_map.44 = f32[2,128,128]{2,1,0:T(8,128)} custom-call(s32[5]{0:T(128)S(1)} %stack.20.place_ref, f32[2,128,128]{2,1,0:T(8,128)S(1)} %copy-done.7, f32[2,128,128]{2,1,0:T(8,128)S(1)} %copy-done.9, f32[2,128,128]{2,1,0:T(8,128)S(1)} %copy-done.12, f32[2,128,128]{2,1,0:T(8,128)S(1)} %copy-done.13, f32[2,128,256]{2,1,0:T(8,128)S(1)} %get-tuple-element.14.rows_ref), custom_call_target="tpu_custom_call" | custom-call | tf_op jit(solution)/shard_map/pallas_call | solution.py:483
  (1 shorter events, 0.0 us)
Async XLA Ops:
  0.7 1.0 %copy-start.10 = (f32[1,1,4,2,64,64]{5,4,3,2,1,0:T(8,128)S(1)}, f32[1,1,4,2,64,64]{5,4,3,2,1,0:T(8,128)}, u32[]{:S(2)}) copy-start(f32[1,1,4,2,64,64]{5,4,3,2,1,0:T(8,128)} %param.4) | copy-start | bytes 393220
  1.6 0.9 %copy-start.11 = (f32[1,1,2,128,128]{4,3,2,1,0:T(8,128)S(1)}, f32[1,1,2,128,128]{4,3,2,1,0:T(8,128)}, u32[]{:S(2)}) copy-start(f32[1,1,2,128,128]{4,3,2,1,0:T(8,128)} %param.3) | copy-start | bytes 393220
  2.5 1.4 %collective-permute-start = (f32[2,128,128]{2,1,0:T(8,128)S(1)}, f32[2,128,128]{2,1,0:T(8,128)S(1)}, u32[]{:S(2)}, u32[]{:S(2)}) collective-permute-start(f32[2,128,128]{2,1,0:T(8,128)S(1)} %shard_map.37.own_ref), channel_id=1, source_target_pairs={{0,1},{1,0},{2,3},{3,2},{4,5},{5,4},{6,7},{7,6},{8,9},{9,8},{10,11... | collective-permute-start | bytes 393224 | tf_op jit(solution)/shard_map/ppermute | solution.py:17
  7.0 0.8 %copy-start.2 = (f32[2,192,192]{2,1,0:T(8,128)}, f32[2,192,192]{2,1,0:T(8,128)S(1)}, u32[]{:S(2)}) copy-start(f32[2,192,192]{2,1,0:T(8,128)S(1)} %shard_map.38.own_ref) | copy-start | bytes 884740
  22.5 1.0 %copy-start.3 = (f32[2,192,192]{2,1,0:T(8,128)S(1)}, f32[2,192,192]{2,1,0:T(8,128)}, u32[]{:S(2)}) copy-start(f32[2,192,192]{2,1,0:T(8,128)} %copy-done.2) | copy-start | bytes 884740
  23.5 1.0 %copy-start.5 = (f32[2,192,192]{2,1,0:T(8,128)S(1)}, f32[2,192,192]{2,1,0:T(8,128)}, u32[]{:S(2)}) copy-start(f32[2,192,192]{2,1,0:T(8,128)} %shard_map.39.partner_ref) | copy-start | bytes 884740
  28.0 0.8 %copy-start = (f32[2,256,256]{2,1,0:T(8,128)}, f32[2,256,256]{2,1,0:T(8,128)S(1)}, u32[]{:S(2)}) copy-start(f32[2,256,256]{2,1,0:T(8,128)S(1)} %shard_map.40.own_ref) | copy-start | bytes 1572868
  40.3 1.0 %copy-start.1 = (f32[2,256,256]{2,1,0:T(8,128)S(1)}, f32[2,256,256]{2,1,0:T(8,128)}, u32[]{:S(2)}) copy-start(f32[2,256,256]{2,1,0:T(8,128)} %copy-done) | copy-start | bytes 1572868
  41.3 1.0 %copy-start.4 = (f32[2,256,256]{2,1,0:T(8,128)S(1)}, f32[2,256,256]{2,1,0:T(8,128)}, u32[]{:S(2)}) copy-start(f32[2,256,256]{2,1,0:T(8,128)} %shard_map.41.partner_ref) | copy-start | bytes 1572868
  46.4 0.7 copy-start.6
  47.0 0.7 copy-start.8
  47.7 14.0 %copy-start.7 = (f32[2,128,128]{2,1,0:T(8,128)S(1)}, f32[2,128,128]{2,1,0:T(8,128)}, u32[]{:S(2)}) copy-start(f32[2,128,128]{2,1,0:T(8,128)} %copy-done.6) | copy-start | bytes 393220
  47.7 14.0 %copy-start.9 = (f32[2,128,128]{2,1,0:T(8,128)S(1)}, f32[2,128,128]{2,1,0:T(8,128)}, u32[]{:S(2)}) copy-start(f32[2,128,128]{2,1,0:T(8,128)} %copy-done.8) | copy-start | bytes 393220
  61.7 0.9 %copy-start.12 = (f32[2,128,128]{2,1,0:T(8,128)S(1)}, f32[2,128,128]{2,1,0:T(8,128)}, u32[]{:S(2)}) copy-start(f32[2,128,128]{2,1,0:T(8,128)} %get-tuple-element.12.got_face_ref) | copy-start | bytes 393220
  62.6 0.9 %copy-start.13 = (f32[2,128,128]{2,1,0:T(8,128)S(1)}, f32[2,128,128]{2,1,0:T(8,128)}, u32[]{:S(2)}) copy-start(f32[2,128,128]{2,1,0:T(8,128)} %get-tuple-element.13.got_outward_ref) | copy-start | bytes 393220
